TPU v7x, 128 devices: a whole 4x4x4 slice. The times are simulated.
128 devices in a mesh: gx: 4 (over z_lo, core), gy: 8 (over z_hi, y), gz: 4 (over x).
Axes of the slice: x: 4, y: 4, z: 4 (z_hi: 2, z_lo: 2; z = z_hi * 2 + z_lo), core: 2. Of those that a mesh axis runs over, the one named last changes fastest.
Arguments:
- cell_volume: float32 [64, 128, 512], P('gx', 'gy', 'gz'), may hold values from 0.5 to 2
- exponent: int32 [64, 128, 512], P('gx', 'gy', 'gz'), may hold values from 0 to 7
- owner_row: int32 [32768], P(('gx', 'gy', 'gz')), may hold values from 0 to 32767, as said below
Outputs:
- stencil_out: float32 [27, 32768, 128], P(None, ('gx', 'gy', 'gz'))
- lumped_out: float32 [32768, 128], P(('gx', 'gy', 'gz'))
Inputs may be any that keep to these rules, and one draw needn't show every extreme that they name: owner_row is a permutation of the row blocks; the row blocks of each device's share of owner_row go to each owner (owner_row // 256) exactly 2 times.
All inputs are finite; a program needn't handle non-finite values.
Results may differ from a plain program's by a relative error of at most 0.00007.
Values sent between devices are 32-bit elements; how exact they have to be, the bound alone decides.
A program may use at most 64 MiB of HBM per device.

v0:
```python
import jax
import jax.numpy as jnp
import numpy as np
from jax import lax
from jax.sharding import PartitionSpec as P

log_step = 0.3


def from_behind(block, axis, distance):
    devices = range(lax.axis_size(axis))
    route = [((i - distance) % len(devices), i) for i in devices]
    return lax.ppermute(block, axis, route)


def weight_table():
    table = np.zeros((27, 8), np.float32)
    for index_o in range(27):
        offsets = (index_o // 9 - 1, index_o // 3 % 3 - 1, index_o % 3 - 1)
        for index_a in range(8):
            corner = (index_a // 4, index_a // 2 % 2, index_a % 2)
            inside = all((0 <= corner[slot_d] + offsets[slot_d] <= 1 for slot_d in range(3)))
            factor = 1.0
            for slot_d in range(3):
                factor = factor * (2.0 if offsets[slot_d] == 0 else 1.0)
            table[index_o, index_a] = factor / 64.0 if inside else 0.0
    return table


def rim_section(current, along, stack_at, sender):
    length = current.shape[along]
    interior = lax.slice_in_dim(current, 0, length - 1, axis=along)
    top_layer = lax.slice_in_dim(current, length - 1, length, axis=along)
    received = sender(top_layer)
    behind = jnp.concatenate([received, interior], axis=along)
    return jnp.stack([current, behind], axis=stack_at)


def shards(cell_volume, exponent, owner_row):
    weight = cell_volume * jnp.exp(-log_step * exponent.astype(jnp.float32))
    span_x, span_y, span_z = weight.shape
    line_count = span_x * span_y
    devices_all = lax.axis_size(("gx", "gy", "gz"))

    def send_z(rim_layer):
        return from_behind(rim_layer, "gz", 1)

    def send_x(rim_layer):
        return from_behind(rim_layer, "gx", 1)

    def send_y(rim_layer):
        return from_behind(rim_layer, "gy", 1)

    owner_dev = owner_row // line_count
    by_owner = jnp.argsort(owner_dev, stable=True)
    slot_ids = (owner_row % line_count)[by_owner].reshape(1, devices_all, -1)
    table = jnp.asarray(weight_table())
    sectioned_z = rim_section(weight, 2, 0, send_z)
    sectioned_x = rim_section(sectioned_z, 1, 0, send_x)
    sectioned_all = rim_section(sectioned_x, 3, 1, send_y)
    corners = sectioned_all.reshape(8, line_count, span_z)
    packed = corners[:, by_owner].reshape(8, devices_all, -1, span_z)
    got_rows, got_slots = (
        lax.all_to_all(packed, ("gx", "gy", "gz"), split_axis=1, concat_axis=1, tiled=True),
        lax.all_to_all(slot_ids, ("gx", "gy", "gz"), split_axis=1, concat_axis=1, tiled=True),
    )
    placing = jnp.argsort(got_slots.reshape(-1))
    placed = got_rows.reshape(8, line_count, span_z)[:, placing]
    stencil_rows = jnp.einsum("oa,alz->olz", table, placed, precision=lax.Precision.HIGHEST)
    lumped_rows = 1.0 / jnp.sum(stencil_rows, axis=0)
    return (stencil_rows, lumped_rows)


def solution(mesh):
    return jax.shard_map(
        shards,
        mesh=mesh,
        in_specs=(P("gx", "gy", "gz"), P("gx", "gy", "gz"), P(("gx", "gy", "gz"))),
        out_specs=(P(None, ("gx", "gy", "gz"), None), P(("gx", "gy", "gz"), None)),
        check_vma=False,
    )
```

profile of v0, /device:TPU:1, one launch (start us, length us, event | category | flops | bytes accessed | tf_op | source)
XLA Modules:
  0.0 70.4 jit_solution(13474387986052149990)
XLA Ops:
  0.6 1.0 %exponential_multiply_fusion = f32[16,16,128]{2,1,0:T(8,128)S(1)} fusion(f32[16,16,128]{2,1,0:T(8,128)} %param.4, s32[16,16,128]{2,1,0:T(8,128)} %param.5), kind=kLoop, calls=%fused_computation.23 | loop fusion | flops 98304 | bytes 393216 | tf_op jit(solution)/shard_map/mul | solution.py:40
  1.6 0.1 slice.30
  1.7 2.1 %collective-permute-start = (f32[16,16,1]{2,1,0:T(8,128)S(1)}, f32[16,16,1]{2,1,0:T(8,128)S(1)}, u32[]{:S(2)}, u32[]{:S(2)}) collective-permute-start(f32[16,16,1]{2,1,0:T(8,128)S(1)} %slice.30), channel_id=1, source_target_pairs={{3,0},{0,1},{1,2},{2,3},{7,4},{4,5},{5,6},{6,7},{11,8},{8,9},{9,10... | collective-permute-start | bytes 3080 | tf_op jit(solution)/shard_map/ppermute | solution.py:13
  3.8 0.7 and_select_fusion
  4.5 3.2 %sort.34 = (s32[256]{0:T(256)}, s32[256]{0:T(256)S(1)}) sort(s32[256]{0:T(256)S(1)} %get-tuple-element.13, s32[256]{0:T(256)S(1)} %iota.8), dimensions={0}, to_apply=%region_0.1 | sort | flops 2048 | bytes 4096 | tf_op jit(solution)/shard_map/jit(argsort)/sort | solution.py:55
  7.7 1.9 %gather_fusion.1 = s32[256]{0:T(256)S(1)} fusion(s32[256]{0:T(256)S(1)} %get-tuple-element.12, s32[1024]{0:T(1024)S(1)} %pad_clamp_fusion.1), kind=kCustom, calls=%fused_computation.1 | custom fusion | bytes 3072 | tf_op jit(solution)/shard_map/gather | solution.py:56
  9.6 0.8 %reshape.22 = s32[1,128,2]{2,1,0:T(8,128)} reshape(s32[256]{0:T(256)S(1)} %gather_fusion.1) | data formatting | bytes 2048 | tf_op jit(solution)/shard_map/reshape | solution.py:56
  10.4 10.7 %all-to-all-start.1 = ((s32[1,128,2]{2,0,1:T(1,128)}), s32[1,128,2]{2,0,1:T(1,128)S(1)}, u32[]{:S(2)}, u32[]{:S(2)}) async-start(s32[1,128,2]{2,0,1:T(1,128)} %bitcast.12), calls=%async_computation.1 | async-start | bytes 131072 | tf_op jit(solution)/shard_map/all_to_all | solution.py:65
  21.1 0.0 collective-permute-done
  21.1 0.1 maximum_bitcast_fusion.2
  21.2 1.8 %collective-permute-start.1 = (f32[2,1,16,128]{3,2,1,0:T(8,128)S(1)}, f32[2,1,16,128]{3,2,1,0:T(8,128)S(1)}, u32[]{:S(2)}, u32[]{:S(2)}) collective-permute-start(f32[2,1,16,128]{3,2,1,0:T(8,128)S(1)} %fusion.7), channel_id=1, source_target_pairs={{96,0},{0,32},{32,64},{64,96},{97,1},{1,33},{33,65},{65,97},{98,2}... | collective-permute-start | bytes 49160 | tf_op jit(solution)/shard_map/ppermute | solution.py:13
  23.1 0.8 %collective-permute-done.1 = f32[2,1,16,128]{3,2,1,0:T(8,128)S(1)} collective-permute-done((f32[2,1,16,128]{3,2,1,0:T(8,128)S(1)}, f32[2,1,16,128]{3,2,1,0:T(8,128)S(1)}, u32[]{:S(2)}, u32[]{:S(2)}) %collective-permute-start.1) | collective-permute-done | bytes 16416 | tf_op jit(solution)/shard_map/ppermute | solution.py:13
  24.0 1.3 %collective-permute-start.2 = (f32[2,2,16,1,128]{4,3,2,1,0:T(1,128)S(1)}, f32[2,2,16,1,128]{4,3,2,1,0:T(1,128)S(1)}, u32[]{:S(2)}, u32[]{:S(2)}) collective-permute-start(f32[2,2,16,1,128]{4,3,2,1,0:T(1,128)S(1)} %fusion.6), channel_id=1, source_target_pairs={{28,0},{0,4},{4,8},{8,12},{12,16},{16,20},{20,24},{24,28},{29,1},{... | collective-permute-start | bytes 98312 | tf_op jit(solution)/shard_map/ppermute | solution.py:13
  25.4 5.6 %collective-permute-done.2 = f32[2,2,16,1,128]{4,3,2,1,0:T(1,128)S(1)} collective-permute-done((f32[2,2,16,1,128]{4,3,2,1,0:T(1,128)S(1)}, f32[2,2,16,1,128]{4,3,2,1,0:T(1,128)S(1)}, u32[]{:S(2)}, u32[]{:S(2)}) %collective-permute-start.2) | collective-permute-done | bytes 32800 | tf_op jit(solution)/shard_map/ppermute | solution.py:13
  31.0 0.1 maximum_bitcast_fusion
  31.0 0.1 pad_maximum_fusion
  31.1 0.0 copy-start
  31.1 0.6 copy.11
  31.7 2.0 %gather_fusion = f32[256,8,128]{2,1,0:T(8,128)} fusion(f32[8,256,128]{2,0,1:T(8,128)S(1)} %copy.11, s32[1024]{0:T(1024)S(1)} %pad_clamp_fusion.1), kind=kCustom, calls=%fused_computation | custom fusion | bytes 2098176 | tf_op jit(solution)/shard_map/gather | solution.py:62
  33.7 0.0 all-to-all-done.1
  33.7 8.5 %all-to-all-start = ((f32[8,128,2,128]{3,0,2,1:T(8,128)}), f32[8,128,2,128]{3,0,2,1:T(8,128)S(1)}, u32[]{:S(2)}, u32[]{:S(2)}) async-start(f32[8,128,2,128]{3,0,2,1:T(8,128)} %bitcast.10), calls=%async_computation | async-start | bytes 2097152 | tf_op jit(solution)/shard_map/all_to_all | solution.py:64
  42.2 0.5 broadcast.50
  42.7 0.8 %reduce.3 = s32[128,2]{1,0:T(8,128)S(1)} reduce(s32[1,128,2]{2,0,1:T(1,128)S(1)} %all-to-all-done.1, s32[]{:T(128)} %broadcast.50), dimensions={0}, to_apply=%all_to_all.7.reduce_sub_computation.3 | reduce | bytes 2052 | tf_op jit(solution)/shard_map/all_to_all | solution.py:65
  43.6 0.1 reshape.23
  43.7 3.2 %sort.35 = (s32[256]{0:T(256)}, s32[256]{0:T(256)S(1)}) sort(s32[256]{0:T(256)S(1)} %reshape.23, s32[256]{0:T(256)S(1)} %iota.9), dimensions={0}, to_apply=%region_1.2 | sort | flops 2048 | bytes 4096 | tf_op jit(solution)/shard_map/jit(argsort)/sort | solution.py:67
  46.9 14.2 %all-to-all-done = f32[8,128,2,128]{3,0,2,1:T(8,128)S(1)} async-done(((f32[8,128,2,128]{3,0,2,1:T(8,128)}), f32[8,128,2,128]{3,0,2,1:T(8,128)S(1)}, u32[]{:S(2)}, u32[]{:S(2)}) %all-to-all-start) | async-done | bytes 1048608 | tf_op jit(solution)/shard_map/all_to_all | solution.py:64
  61.1 1.0 %gather_fusion.2 = f32[256,8,128]{2,1,0:T(8,128)S(1)} fusion(f32[8,256,128]{2,0,1:T(8,128)S(1)} %bitcast.33, s32[1024]{0:T(1024)S(1)} %pad_clamp_fusion), kind=kCustom, calls=%fused_computation.2 | custom fusion | bytes 2098176 | tf_op jit(solution)/shard_map/gather | solution.py:68
  62.1 0.0 copy-done
  62.1 3.7 %fusion.8 = (f32[256,128]{1,0:T(8,128)S(1)}, f32[27,256,128]{2,0,1:T(8,128)S(1)}) fusion(f32[27,8,1]{0,1,2:T(8,128)S(1)} %copy-done, f32[256,8,128]{2,1,0:T(8,128)S(1)} %gather_fusion.2), kind=kOutput, calls=%fused_computation.38 | convolution fusion | flops 85786624 | bytes 4719456 | tf_op jit(solution)/shard_map/oa,alz->olz/dot_general | solution.py:69
  65.9 0.7 broadcast_divide_fusion
  66.5 3.8 %copy.13 = f32[27,256,128]{2,1,0:T(8,128)} copy(f32[27,256,128]{2,0,1:T(8,128)S(1)} %get-tuple-element.15) | data formatting | bytes 7077888
  (13 shorter events, 0.2 us)
Async XLA Ops:
  1.7 19.4 %collective-permute-start = (f32[16,16,1]{2,1,0:T(8,128)S(1)}, f32[16,16,1]{2,1,0:T(8,128)S(1)}, u32[]{:S(2)}, u32[]{:S(2)}) collective-permute-start(f32[16,16,1]{2,1,0:T(8,128)S(1)} %slice.30), channel_id=1, source_target_pairs={{3,0},{0,1},{1,2},{2,3},{7,4},{4,5},{5,6},{6,7},{11,8},{8,9},{9,10... | collective-permute-start | bytes 3080 | tf_op jit(solution)/shard_map/ppermute | solution.py:13
  10.4 23.3 %all-to-all-start.1 = ((s32[1,128,2]{2,0,1:T(1,128)}), s32[1,128,2]{2,0,1:T(1,128)S(1)}, u32[]{:S(2)}, u32[]{:S(2)}) async-start(s32[1,128,2]{2,0,1:T(1,128)} %bitcast.12), calls=%async_computation.1 | async-start | bytes 131072 | tf_op jit(solution)/shard_map/all_to_all | solution.py:65
  21.2 2.7 %collective-permute-start.1 = (f32[2,1,16,128]{3,2,1,0:T(8,128)S(1)}, f32[2,1,16,128]{3,2,1,0:T(8,128)S(1)}, u32[]{:S(2)}, u32[]{:S(2)}) collective-permute-start(f32[2,1,16,128]{3,2,1,0:T(8,128)S(1)} %fusion.7), channel_id=1, source_target_pairs={{96,0},{0,32},{32,64},{64,96},{97,1},{1,33},{33,65},{65,97},{98,2}... | collective-permute-start | bytes 49160 | tf_op jit(solution)/shard_map/ppermute | solution.py:13
  24.0 6.9 %collective-permute-start.2 = (f32[2,2,16,1,128]{4,3,2,1,0:T(1,128)S(1)}, f32[2,2,16,1,128]{4,3,2,1,0:T(1,128)S(1)}, u32[]{:S(2)}, u32[]{:S(2)}) collective-permute-start(f32[2,2,16,1,128]{4,3,2,1,0:T(1,128)S(1)} %fusion.6), channel_id=1, source_target_pairs={{28,0},{0,4},{4,8},{8,12},{12,16},{16,20},{20,24},{24,28},{29,1},{... | collective-permute-start | bytes 98312 | tf_op jit(solution)/shard_map/ppermute | solution.py:13
  31.1 31.0 %copy-start = (f32[27,8,1]{0,1,2:T(8,128)S(1)}, f32[27,8,1]{0,1,2:T(8,128)}, u32[]{:S(2)}) copy-start(f32[27,8,1]{0,1,2:T(8,128)} %constant.39) | copy-start | bytes 2596
  33.7 27.3 %all-to-all-start = ((f32[8,128,2,128]{3,0,2,1:T(8,128)}), f32[8,128,2,128]{3,0,2,1:T(8,128)S(1)}, u32[]{:S(2)}, u32[]{:S(2)}) async-start(f32[8,128,2,128]{3,0,2,1:T(8,128)} %bitcast.10), calls=%async_computation | async-start | bytes 2097152 | tf_op jit(solution)/shard_map/all_to_all | solution.py:64
where the time goes:
time: 70.6 us; the launch traced here: 70.4 us
  starting transfers between devices  24.4 us (35%)
  waiting for transfers between devices  20.6 us (29%)
  local copies, waits for them, and re-layouts  10.9 us (15%)
  other arithmetic  9.93 us (14%)
  matrix products  3.73 us (5%)
  between operations  0.8 us (1%)
    all_to_all x1, waiting for transfers between devices, shards(): lax.all_to_all(packed, ('gx', 'gy', 'gz'), split_axis=1, concat_axis=1, t...  14.2 us
    all_to_all x1, starting transfers between devices, shards(): lax.all_to_all(slot_ids, ('gx', 'gy', 'gz'), split_axis=1, concat_axis=1,...  10.7 us
    all_to_all x1, starting transfers between devices, shards(): lax.all_to_all(packed, ('gx', 'gy', 'gz'), split_axis=1, concat_axis=1, t...  8.48 us
    ppermute x3, waiting for transfers between devices, from_behind(): return lax.ppermute(block, axis, route)  6.43 us
    ppermute x3, starting transfers between devices, from_behind(): return lax.ppermute(block, axis, route)  5.24 us
    unnamed x3, local copies, waits for them, and re-layouts  3.85 us
    dot_general x1, matrix products, shards(): jnp.einsum('oa,alz->olz', table, placed, precision=lax.Precision.HIGHEST)  3.73 us
    sort x1, other arithmetic, shards(): by_owner = jnp.argsort(owner_dev, stable=True)  3.17 us
  transfers between devices with their start and end apart: 5, of which 3 were waited for; matrix products, arithmetic and copies ran while one was open for 20% of the time, Pallas kernels for 0%

commit v1 on v0

v1 whole, which is shorter than its diff:
```python
import jax
import jax.numpy as jnp
from jax import lax
from jax.experimental import pallas as pl
from jax.experimental.pallas import tpu as pltpu
from jax.sharding import PartitionSpec as P

MESH = pl.DeviceIdType.MESH
AXES = ("gx", "gy", "gz")
LOG_STEP = 0.3
NX, NY, NZ = 4, 8, 4
DEV = NX * NY * NZ
SPAN = 16
ROWS = SPAN * SPAN
LANES = 128
PARTS = 5
CHUNKS = 4
HALO = ((1, 0, 0), (0, 1, 0), (1, 1, 0), (0, 0, 1), (1, 0, 1), (0, 1, 1), (1, 1, 1))

f32, bf16, i32 = jnp.float32, jnp.bfloat16, jnp.int32


def pieces(x):
    high = x.astype(bf16)
    rest = x - high.astype(f32)
    middle = rest.astype(bf16)
    low = (rest - middle.astype(f32)).astype(bf16)
    return high, middle, low


def dot_t(a, b):
    return lax.dot_general(a, b, (((1,), (1,)), ((), ())), preferred_element_type=f32)


def dot_n(a, b):
    return lax.dot_general(a, b, (((1,), (0,)), ((), ())), preferred_element_type=f32)


def pick(select, x):
    return sum(dot_n(select, piece) for piece in pieces(x))


def pick_t(select, x):
    return sum(dot_t(select, piece) for piece in pieces(x))


def exchange(
    volume_hbm, exponent_hbm, owner_hbm, got,
    volume, exponent, owner, weight, y_layer, edge,
    x_got, y_got, xy_got, z_got, packed,
    in_sems, halo_send, halo_recv, send_sem, recv_sem, own_sem,
):
    me = tuple(lax.axis_index(axis) for axis in AXES)
    my_dev = (me[0] * NY + me[1]) * NZ + me[2]

    def ahead(x, y, z):
        return (lax.rem(me[0] + x, NX), lax.rem(me[1] + y, NY), lax.rem(me[2] + z, NZ))

    def peer(step):
        return ahead(step // (NY * NZ), lax.rem(step // NZ, NY), lax.rem(step, NZ))

    loads = [
        pltpu.make_async_copy(src, dst, in_sems.at[n])
        for n, (src, dst) in enumerate(
            ((volume_hbm, volume), (exponent_hbm, exponent), (owner_hbm, owner))
        )
    ]
    for load in loads:
        load.start()

    barrier = pltpu.get_barrier_semaphore()

    def greet(step, carry):
        pl.semaphore_signal(barrier, inc=1, device_id=peer(step), device_id_type=MESH)
        return carry

    lax.fori_loop(1, DEV, greet, 0)

    for load in loads:
        load.wait()
    weight[...] = volume[...] * jnp.exp(-LOG_STEP * exponent[...].astype(f32))
    y_layer[...] = weight[pl.ds(SPAN - 1, SPAN, stride=SPAN), :]
    last = (lax.broadcasted_iota(i32, (8, LANES), 1) == LANES - 1).astype(bf16)
    edge[...] = pick_t(last, weight[...])[0:1]

    rows = lax.broadcasted_iota(i32, (ROWS, ROWS), 0)
    columns = lax.broadcasted_iota(i32, (ROWS, ROWS), 1)
    owner_dev = owner[...] // ROWS
    slots = (owner[...] - owner_dev * ROWS).astype(f32)
    same = owner_dev == rows // 2
    before = (rows < columns).astype(bf16)
    rank = dot_n(same.astype(bf16), before)
    order = jnp.where(same & (rank == (rows % 2).astype(f32)), 1.0, 0.0).astype(bf16)

    pl.semaphore_wait(barrier, DEV - 1)
    sources = (
        weight.at[pl.ds(ROWS - SPAN, SPAN)], y_layer, weight.at[pl.ds(ROWS - 8, 8)],
        edge, edge, edge, edge,
    )
    targets = (x_got, y_got, xy_got, z_got.at[0], z_got.at[1], z_got.at[2], z_got.at[3])
    halos = []
    for n, step in enumerate(HALO):
        copy = pltpu.make_async_remote_copy(
            src_ref=sources[n], dst_ref=targets[n],
            send_sem=halo_send.at[n], recv_sem=halo_recv.at[n],
            device_id=ahead(*step), device_id_type=MESH,
        )
        copy.start()
        halos.append(copy)

    packed[0] = pick(order, weight[...]).reshape(DEV, 2, LANES)
    for copy in halos:
        copy.wait()

    own = weight[...].reshape(SPAN, SPAN, LANES)
    x_layer, y_back = x_got[...], y_got[...]
    corner = xy_got[7:8]
    behind_x = jnp.concatenate([x_layer[None], own[:-1]], axis=0)
    behind_y = jnp.concatenate([y_back[:, None], own[:, :-1]], axis=1)
    y_edge = jnp.concatenate([corner, y_back[:-1]], axis=0)
    behind_xy = jnp.concatenate([y_edge[:, None], behind_x[:, :-1]], axis=1)
    for n, lines in enumerate((behind_x, behind_y, behind_xy)):
        packed[n + 1] = pick(order, lines.reshape(ROWS, LANES)).reshape(DEV, 2, LANES)

    at = lax.broadcasted_iota(i32, (1, ROWS), 1)
    first_x, first_y = at < SPAN, at % SPAN == 0
    z_own, z_x, z_y, z_xy = (z_got[n] for n in range(4))

    def turn(row, by):
        return pltpu.roll(row, by % ROWS, 1)

    z_rows = (
        z_own,
        jnp.where(first_x, turn(z_x, SPAN), turn(z_own, SPAN)),
        jnp.where(first_y, turn(z_y, 1 - SPAN), turn(z_own, 1)),
        jnp.where(
            first_x,
            jnp.where(first_y, turn(z_xy, 1), turn(z_x, SPAN + 1)),
            jnp.where(first_y, turn(z_y, 1), turn(z_own, SPAN + 1)),
        ),
        slots,
    )
    line = lax.broadcasted_iota(i32, (LANES, ROWS), 0)
    table = jnp.zeros((LANES, ROWS), f32)
    for n, row in enumerate(z_rows):
        table = jnp.where(line == n, jnp.broadcast_to(row, (LANES, ROWS)), table)
    packed[4] = pick_t(order, table).reshape(DEV, 2, LANES)

    def send(step):
        there = peer(step)
        dev = (there[0] * NY + there[1]) * NZ + there[2]
        return pltpu.make_async_remote_copy(
            src_ref=packed.at[:, dev], dst_ref=got.at[:, my_dev],
            send_sem=send_sem, recv_sem=recv_sem,
            device_id=there, device_id_type=MESH,
        )

    def start(n, carry):
        send(lax.rem(n * 37, DEV)).start()
        return carry

    lax.fori_loop(1, DEV, start, 0)
    keep = pltpu.make_async_copy(packed.at[:, my_dev], got.at[:, my_dev], own_sem)
    keep.start()
    keep.wait()

    all_others = pl.ds(0, DEV - 1)
    pltpu.make_async_remote_copy(
        src_ref=packed.at[:, all_others], dst_ref=got.at[:, all_others],
        send_sem=send_sem, recv_sem=recv_sem, device_id=me, device_id_type=MESH,
    ).wait()


def assemble(got, stencil_hbm, lumped_hbm, stencil, lumped, out_sems, lump_sem):
    rows = ROWS // CHUNKS
    extra = got[4].reshape(ROWS, LANES)
    fourth = (lax.broadcasted_iota(i32, (8, LANES), 1) == 4).astype(bf16)
    slot = dot_t(fourth, extra.astype(bf16))[0:1]
    line_pieces = [pieces(got[n].reshape(ROWS, LANES)) for n in range(PARTS)]
    lane = lax.broadcasted_iota(i32, (rows, LANES), 1)
    copies = []
    for chunk in range(CHUNKS):
        here = pl.ds(chunk * rows, rows)
        mine = lax.broadcasted_iota(i32, (rows, ROWS), 0) + chunk * rows
        place = jnp.where(slot == mine.astype(f32), 1.0, 0.0).astype(bf16)
        placed = [sum(dot_n(place, piece) for piece in three) for three in line_pieces]
        lines, tail = placed[:4], placed[4]
        now = [line * 0.015625 for line in lines]
        behind = [
            jnp.where(lane == 0, tail[:, n : n + 1] * 0.015625, pltpu.roll(line, 1, 1))
            for n, line in enumerate(now)
        ]
        total = sum(now) + sum(behind)
        lumped[here, :] = 1.0 / (27.0 * total)

        def spread(current, back):
            return (back, 2.0 * (current + back), current)

        def plane(four):
            along = zip(spread(four[0], four[1]), spread(four[2], four[3]))
            return [value for current, back in along for value in spread(current, back)]

        for n, (current, back) in enumerate(zip(plane(now), plane(behind))):
            for k, value in enumerate(spread(current, back)):
                stencil[3 * n + k, here, :] = value
        copy = pltpu.make_async_copy(
            stencil.at[:, here], stencil_hbm.at[:, here], out_sems.at[chunk]
        )
        copy.start()
        copies.append(copy)
    copy = pltpu.make_async_copy(lumped, lumped_hbm, lump_sem)
    copy.start()
    copies.append(copy)
    for copy in copies:
        copy.wait()


def shards(cell_volume, exponent, owner_row):
    vmem = pl.BlockSpec(memory_space=pltpu.VMEM)
    hbm = pl.BlockSpec(memory_space=pltpu.HBM)
    dma = pltpu.SemaphoreType.DMA
    got = pl.pallas_call(
        exchange,
        name="exchange",
        out_shape=jax.ShapeDtypeStruct((PARTS, DEV, 2, LANES), f32),
        in_specs=[hbm] * 3,
        out_specs=vmem,
        scratch_shapes=[
            pltpu.VMEM((ROWS, LANES), f32),
            pltpu.VMEM((ROWS, LANES), i32),
            pltpu.VMEM((1, ROWS), i32),
            pltpu.VMEM((ROWS, LANES), f32),
            pltpu.VMEM((SPAN, LANES), f32),
            pltpu.VMEM((1, ROWS), f32),
            pltpu.VMEM((SPAN, LANES), f32),
            pltpu.VMEM((SPAN, LANES), f32),
            pltpu.VMEM((8, LANES), f32),
            pltpu.VMEM((4, 1, ROWS), f32),
            pltpu.VMEM((PARTS, DEV, 2, LANES), f32),
            dma((3,)), dma((7,)), dma((7,)), dma, dma, dma,
        ],
        compiler_params=pltpu.CompilerParams(has_side_effects=True, collective_id=1),
    )(
        cell_volume.reshape(ROWS, LANES),
        exponent.reshape(ROWS, LANES),
        owner_row.reshape(1, ROWS),
    )
    return pl.pallas_call(
        assemble,
        name="assemble",
        out_shape=(
            jax.ShapeDtypeStruct((27, ROWS, LANES), f32),
            jax.ShapeDtypeStruct((ROWS, LANES), f32),
        ),
        in_specs=[vmem],
        out_specs=(hbm, hbm),
        scratch_shapes=[
            pltpu.VMEM((27, ROWS, LANES), f32),
            pltpu.VMEM((ROWS, LANES), f32),
            dma((CHUNKS,)), dma,
        ],
    )(got)


def solution(mesh):
    return jax.shard_map(
        shards,
        mesh=mesh,
        in_specs=(P(*AXES), P(*AXES), P(AXES)),
        out_specs=(P(None, AXES, None), P(AXES, None)),
        check_vma=False,
    )
```

time: 70.6 us -> 33.8 us (0.48)
  Pallas kernels: 0 us -> 33 us
  starting transfers between devices: 24.4 us -> 0 us
  waiting for transfers between devices: 20.6 us -> 0 us
  local copies, waits for them, and re-layouts: 10.9 us -> 0 us
  other arithmetic: 9.93 us -> 0 us
  matrix products: 3.73 us -> 0 us
    pallas_call x0 -> x2, Pallas kernels: none -> 33 us  [the longest x1 28.9 us: shards(): pl.pallas_call(exchange, name='exchange', out_shape=jax.ShapeDtypeStruct(...]
    all_to_all x2 -> x0, starting transfers between devices: 19.1 us -> none  [the longest x1 10.7 us: shards(): lax.all_to_all(slot_ids, ('gx', 'gy', 'gz'), split_axis=1, concat_axis=1,...]
    all_to_all x2 -> x0, waiting for transfers between devices: 14.2 us -> none  [the longest x1 14.2 us: shards(): lax.all_to_all(packed, ('gx', 'gy', 'gz'), split_axis=1, concat_axis=1, t...]
    ppermute x3 -> x0, waiting for transfers between devices: 6.43 us -> none  [from_behind(): return lax.ppermute(block, axis, route)]
    sort x2 -> x0, other arithmetic: 6.33 us -> none  [the longest x1 3.17 us: shards(): by_owner = jnp.argsort(owner_dev, stable=True)]
    ppermute x3 -> x0, starting transfers between devices: 5.24 us -> none  [from_behind(): return lax.ppermute(block, axis, route)]
    gather x3 -> x0, local copies, waits for them, and re-layouts: 4.96 us -> none  [the longest x1 2 us: shards(): packed = corners[:, by_owner].reshape(8, devices_all, -1, span_z)]
    unnamed x3 -> x0, local copies, waits for them, and re-layouts: 3.85 us -> none
  transfers between devices with their start and end apart: 5 -> 0, of which waited for: 3 -> 0; matrix products, arithmetic and copies ran while one was open for 20% -> 0% of each run, Pallas kernels for 0% -> 0%
where the time goes in v1:
time: 33.8 us; the launch traced here: 33.7 us
  Pallas kernels  33 us (98%)
  between operations  0.64 us (2%)
    pallas_call x1, Pallas kernels, shards(): pl.pallas_call(exchange, name='exchange', out_shape=jax.ShapeDtypeStruct(...  28.9 us
    pallas_call x1, Pallas kernels, shards(): pl.pallas_call(assemble, name='assemble', out_shape=(jax.ShapeDtypeStruct...  4.12 us

profile of v1, /device:TPU:1, one launch (start us, length us, event | category | flops | bytes accessed | tf_op | source)
XLA Modules:
  0.0 33.7 jit_solution(18362966051895558258)
XLA Ops:
  0.6 28.9 %exchange.1.got = f32[5,128,2,128]{3,2,1,0:T(2,128)} custom-call(f32[256,128]{1,0:T(8,128)} %bitcast.3, s32[256,128]{1,0:T(8,128)} %bitcast.4, s32[1,256]{1,0:T(1,128)} %bitcast.5), custom_call_target="tpu_custom_call" | custom-call | tf_op jit(solution)/shard_map/exchange/pallas_call | solution.py:222
  29.5 4.1 %assemble.1 = (f32[27,256,128]{2,1,0:T(8,128)}, f32[256,128]{1,0:T(8,128)}) custom-call(f32[5,128,2,128]{3,2,1,0:T(2,128)} %exchange.1.got), custom_call_target="tpu_custom_call" | custom-call | tf_op jit(solution)/shard_map/assemble/pallas_call | solution.py:248

commit v2 on v1

--- a/solution.py
+++ b/solution.py
@@ -5,7 +5,7 @@
 from jax.experimental.pallas import tpu as pltpu
 from jax.sharding import PartitionSpec as P
 
-MESH = pl.DeviceIdType.MESH
+LOGICAL = pl.DeviceIdType.LOGICAL
 AXES = ("gx", "gy", "gz")
 LOG_STEP = 0.3
 NX, NY, NZ = 4, 8, 4
@@ -15,6 +15,7 @@
 LANES = 128
 PARTS = 5
 CHUNKS = 4
+ROOT = (3 * NY + 6) * NZ + 2
 HALO = ((1, 0, 0), (0, 1, 0), (1, 1, 0), (0, 0, 1), (1, 0, 1), (0, 1, 1), (1, 1, 1))
 
 f32, bf16, i32 = jnp.float32, jnp.bfloat16, jnp.int32
@@ -48,16 +49,22 @@
     volume_hbm, exponent_hbm, owner_hbm, got,
     volume, exponent, owner, weight, y_layer, edge,
     x_got, y_got, xy_got, z_got, packed,
-    in_sems, halo_send, halo_recv, send_sem, recv_sem, own_sem,
+    in_sems, halo_send, halo_recv, send_sem, recv_sem, own_sem, go_sem,
 ):
     me = tuple(lax.axis_index(axis) for axis in AXES)
-    my_dev = (me[0] * NY + me[1]) * NZ + me[2]
+    along_x = [lax.rem(me[0] + k, NX) * (NY * NZ) for k in range(NX)]
+    along_y = [lax.rem(me[1] + k, NY) * NZ for k in range(NY)]
+    along_z = [lax.rem(me[2] + k, NZ) for k in range(NZ)]
+    my_dev = along_x[0] + along_y[0] + along_z[0]
+    is_root = my_dev == ROOT
 
     def ahead(x, y, z):
-        return (lax.rem(me[0] + x, NX), lax.rem(me[1] + y, NY), lax.rem(me[2] + z, NZ))
-
-    def peer(step):
-        return ahead(step // (NY * NZ), lax.rem(step // NZ, NY), lax.rem(step, NZ))
+        return along_x[x % NX] + along_y[y % NY] + along_z[z % NZ]
+
+    others = [
+        ahead(step // (NY * NZ), step // NZ, step)
+        for step in ((n * 37) % DEV for n in range(1, DEV))
+    ]
 
     loads = [
         pltpu.make_async_copy(src, dst, in_sems.at[n])
@@ -70,11 +77,15 @@
 
     barrier = pltpu.get_barrier_semaphore()
 
-    def greet(step, carry):
-        pl.semaphore_signal(barrier, inc=1, device_id=peer(step), device_id_type=MESH)
-        return carry
-
-    lax.fori_loop(1, DEV, greet, 0)
+    greeted = jnp.int32(0)
+    for x, y, z in HALO:
+        source = ahead(-x, -y, -z)
+        pl.semaphore_signal(barrier, inc=1, device_id=source, device_id_type=LOGICAL)
+        greeted = greeted + (source == ROOT).astype(i32)
+
+    @pl.when(jnp.logical_not(is_root) & (greeted == 0))
+    def _():
+        pl.semaphore_signal(barrier, inc=1, device_id=jnp.int32(ROOT), device_id_type=LOGICAL)
 
     for load in loads:
         load.wait()
@@ -92,7 +103,14 @@
     rank = dot_n(same.astype(bf16), before)
     order = jnp.where(same & (rank == (rows % 2).astype(f32)), 1.0, 0.0).astype(bf16)
 
-    pl.semaphore_wait(barrier, DEV - 1)
+    @pl.when(is_root)
+    def _():
+        pl.semaphore_wait(barrier, DEV - 1)
+
+    @pl.when(jnp.logical_not(is_root))
+    def _():
+        pl.semaphore_wait(barrier, len(HALO))
+
     sources = (
         weight.at[pl.ds(ROWS - SPAN, SPAN)], y_layer, weight.at[pl.ds(ROWS - 8, 8)],
         edge, edge, edge, edge,
@@ -103,10 +121,15 @@
         copy = pltpu.make_async_remote_copy(
             src_ref=sources[n], dst_ref=targets[n],
             send_sem=halo_send.at[n], recv_sem=halo_recv.at[n],
-            device_id=ahead(*step), device_id_type=MESH,
+            device_id=ahead(*step), device_id_type=LOGICAL,
         )
         copy.start()
         halos.append(copy)
+
+    @pl.when(is_root)
+    def _():
+        for there in others:
+            pl.semaphore_signal(go_sem, inc=1, device_id=there, device_id_type=LOGICAL)
 
     packed[0] = pick(order, weight[...]).reshape(DEV, 2, LANES)
     for copy in halos:
@@ -146,20 +169,16 @@
         table = jnp.where(line == n, jnp.broadcast_to(row, (LANES, ROWS)), table)
     packed[4] = pick_t(order, table).reshape(DEV, 2, LANES)
 
-    def send(step):
-        there = peer(step)
-        dev = (there[0] * NY + there[1]) * NZ + there[2]
-        return pltpu.make_async_remote_copy(
-            src_ref=packed.at[:, dev], dst_ref=got.at[:, my_dev],
+    @pl.when(jnp.logical_not(is_root))
+    def _():
+        pl.semaphore_wait(go_sem, 1)
+
+    for there in others:
+        pltpu.make_async_remote_copy(
+            src_ref=packed.at[:, there], dst_ref=got.at[:, my_dev],
             send_sem=send_sem, recv_sem=recv_sem,
-            device_id=there, device_id_type=MESH,
-        )
-
-    def start(n, carry):
-        send(lax.rem(n * 37, DEV)).start()
-        return carry
-
-    lax.fori_loop(1, DEV, start, 0)
+            device_id=there, device_id_type=LOGICAL,
+        ).start()
     keep = pltpu.make_async_copy(packed.at[:, my_dev], got.at[:, my_dev], own_sem)
     keep.start()
     keep.wait()
@@ -167,7 +186,7 @@
     all_others = pl.ds(0, DEV - 1)
     pltpu.make_async_remote_copy(
         src_ref=packed.at[:, all_others], dst_ref=got.at[:, all_others],
-        send_sem=send_sem, recv_sem=recv_sem, device_id=me, device_id_type=MESH,
+        send_sem=send_sem, recv_sem=recv_sem, device_id=my_dev, device_id_type=LOGICAL,
     ).wait()
 
 
@@ -215,6 +234,10 @@
         copy.wait()
 
 
+def in_hbm(x):
+    return pltpu.with_memory_space_constraint(x, pltpu.HBM)
+
+
 def shards(cell_volume, exponent, owner_row):
     vmem = pl.BlockSpec(memory_space=pltpu.VMEM)
     hbm = pl.BlockSpec(memory_space=pltpu.HBM)
@@ -222,7 +245,7 @@
     got = pl.pallas_call(
         exchange,
         name="exchange",
-        out_shape=jax.ShapeDtypeStruct((PARTS, DEV, 2, LANES), f32),
+        out_shape=pltpu.VMEM((PARTS, DEV, 2, LANES), f32),
         in_specs=[hbm] * 3,
         out_specs=vmem,
         scratch_shapes=[
@@ -237,13 +260,13 @@
             pltpu.VMEM((8, LANES), f32),
             pltpu.VMEM((4, 1, ROWS), f32),
             pltpu.VMEM((PARTS, DEV, 2, LANES), f32),
-            dma((3,)), dma((7,)), dma((7,)), dma, dma, dma,
+            dma((3,)), dma((7,)), dma((7,)), dma, dma, dma, pltpu.SemaphoreType.REGULAR,
         ],
-        compiler_params=pltpu.CompilerParams(has_side_effects=True, collective_id=1),
+        compiler_params=pltpu.CompilerParams(has_side_effects=True, collective_id=1, vmem_limit_bytes=16 << 20),
     )(
-        cell_volume.reshape(ROWS, LANES),
-        exponent.reshape(ROWS, LANES),
-        owner_row.reshape(1, ROWS),
+        in_hbm(cell_volume.reshape(ROWS, LANES)),
+        in_hbm(exponent.reshape(ROWS, LANES)),
+        in_hbm(owner_row.reshape(1, ROWS)),
     )
     return pl.pallas_call(
         assemble,
@@ -259,6 +282,7 @@
             pltpu.VMEM((ROWS, LANES), f32),
             dma((CHUNKS,)), dma,
         ],
+        compiler_params=pltpu.CompilerParams(vmem_limit_bytes=16 << 20),
     )(got)
 
 

time: 33.8 us -> 27.2 us (0.80); the launches traced: 33.7 us -> 26.7 us
  Pallas kernels: 33 us -> 26 us
    pallas_call x1, Pallas kernels: 28.9 us -> 23 us  [shards(): pl.pallas_call(exchange, name='exchange', out_shape=pltpu.VMEM((PARTS, DE...]
    pallas_call x1, Pallas kernels: 4.12 us -> 3.04 us  [shards(): pl.pallas_call(assemble, name='assemble', out_shape=(jax.ShapeDtypeStruct...]
where the time goes in v2:
time: 27.2 us; the launch traced here: 26.7 us
  Pallas kernels  26 us (96%)
  between operations  0.64 us (2%)
    pallas_call x1, Pallas kernels, shards(): pl.pallas_call(exchange, name='exchange', out_shape=pltpu.VMEM((PARTS, DE...  23 us
    pallas_call x1, Pallas kernels, shards(): pl.pallas_call(assemble, name='assemble', out_shape=(jax.ShapeDtypeStruct...  3.04 us

profile of v2, /device:TPU:1, one launch (start us, length us, event | category | flops | bytes accessed | tf_op | source)
XLA Modules:
  0.0 26.7 jit_solution(6612899654809785390)
XLA Ops:
  0.6 23.0 %exchange.1.got = f32[5,128,2,128]{3,2,1,0:T(2,128)S(1)} custom-call(f32[256,128]{1,0:T(8,128)} %bitcast.3, s32[256,128]{1,0:T(8,128)} %bitcast.4, s32[1,256]{1,0:T(1,128)} %bitcast.5), custom_call_target="tpu_custom_call" | custom-call | tf_op jit(solution)/shard_map/exchange/pallas_call | solution.py:245
  23.6 3.0 %assemble.1 = (f32[27,256,128]{2,1,0:T(8,128)}, f32[256,128]{1,0:T(8,128)}) custom-call(f32[5,128,2,128]{3,2,1,0:T(2,128)S(1)} %exchange.1.got), custom_call_target="tpu_custom_call" | custom-call | tf_op jit(solution)/shard_map/assemble/pallas_call | solution.py:271

commit v3 on v2

v3 whole, which is shorter than its diff:
```python
import jax
import jax.numpy as jnp
from jax import lax
from jax.experimental import pallas as pl
from jax.experimental.pallas import tpu as pltpu
from jax.sharding import PartitionSpec as P

LOGICAL = pl.DeviceIdType.LOGICAL
AXES = ("gx", "gy", "gz")
LOG_STEP = 0.3
NX, NY, NZ = 4, 8, 4
DEV = NX * NY * NZ
HALF = NY // 2
PLANES = 4
ROOT = (3 * NY + 6) * NZ + 2
EARLY_ROOT = (3 * NY + 2) * NZ + 2
MID_ROOT = (0 * NY + 6) * NZ + 2
FIRST = (NY * NZ, 0)
SPAN = 16
ROWS = SPAN * SPAN
LANES = 128
PARTS = 9
CHUNKS = 4
HALO = ((1, 0, 0), (0, 1, 0), (1, 1, 0), (0, 0, 1), (1, 0, 1), (0, 1, 1), (1, 1, 1))

f32, bf16, i32 = jnp.float32, jnp.bfloat16, jnp.int32


def pieces(x):
    high = x.astype(bf16)
    return high, (x - high.astype(f32)).astype(bf16)


def dot_t(a, b):
    return lax.dot_general(a, b, (((1,), (1,)), ((), ())), preferred_element_type=f32)


def dot_n(a, b):
    return lax.dot_general(a, b, (((1,), (0,)), ((), ())), preferred_element_type=f32)


def pick(select, x):
    both = dot_n(select, jnp.concatenate(pieces(x), axis=1))
    return both[:, :LANES] + both[:, LANES:]


def pick_t(select, x):
    return sum(dot_t(select, piece) for piece in pieces(x))


def iota(shape, axis):
    return lax.broadcasted_iota(i32, shape, axis)


def one_hot(mask, value=1.0):
    return jnp.where(mask, value, 0.0).astype(bf16)


def exchange(
    volume_hbm, exponent_hbm, owner_hbm, got,
    volume, exponent, owner, weight, y_layer, edge,
    lines_got, z_got, packed,
    in_sems, halo_send, halo_recv, send_sem, recv_sem, own_sem, go_sem, mid_sem, early_sem,
):
    loads = [
        pltpu.make_async_copy(src, dst, in_sems.at[n])
        for n, (src, dst) in enumerate(
            ((volume_hbm, volume), (exponent_hbm, exponent), (owner_hbm, owner))
        )
    ]
    for load in loads:
        load.start()

    me = tuple(lax.axis_index(axis) for axis in AXES)
    my_dev = (me[0] * NY + me[1]) * NZ + me[2]
    is_root, is_mid_root, is_early_root = (
        my_dev == root for root in (ROOT, MID_ROOT, EARLY_ROOT)
    )
    my_plane = me[0] // 2 + 2 * (me[1] // HALF)
    is_early, is_mid, is_late = my_plane < 2, my_plane == 2, my_plane == 3
    not_ = jnp.logical_not

    def ahead(x, y, z):
        there_x = lax.rem(me[0] + x % NX, NX)
        there_y = lax.rem(me[1] + y % NY, NY)
        there_z = lax.rem(me[2] + z % NZ, NZ)
        return (there_x * NY + there_y) * NZ + there_z

    def signal(sem, there):
        pl.semaphore_signal(sem, inc=1, device_id=there, device_id_type=LOGICAL)

    barrier = pltpu.get_barrier_semaphore()
    sources = [ahead(-x, -y, -z) for x, y, z in HALO]
    def greet(root, wanted):
        known = sum((source == root).astype(i32) for source in sources)

        @pl.when(wanted & (my_dev != root) & (known == 0))
        def _():
            signal(barrier, jnp.int32(root))

    greet(ROOT, my_dev >= 0)
    greet(MID_ROOT, not_(is_late))
    greet(EARLY_ROOT, is_early)
    for source in sources:
        signal(barrier, source)

    def plane(number):
        z_hi, z_lo = number // 2, number % 2
        core, y = lax.rem(me[0], 2), lax.rem(me[1], HALF)
        base_x = [(z_lo * 2 + lax.rem(core + k, 2)) * (NY * NZ) for k in range(2)]
        base_y = [(z_hi * HALF + lax.rem(y + k, HALF)) * NZ for k in range(HALF)]
        base_z = [lax.rem(me[2] + k, NZ) for k in range(NZ)]
        members = 2 * HALF * NZ
        here = my_plane == number
        for n in range(members):
            step = n * 13 % members
            there = base_x[step % 2] + base_y[step // 2 % HALF] + base_z[step // (2 * HALF)]
            yield (here if step == 0 else None), there

    def visit(planes, act, first=()):
        for there in first:
            pl.when(my_dev != there)(lambda: act(jnp.int32(there)))
        for number in planes:
            for self_at, there in plane(number):
                go = None if self_at is None else not_(self_at)
                if number == 0:
                    for known in first:
                        go = there != known if go is None else go & (there != known)
                if go is None:
                    act(there)
                else:
                    pl.when(go)(lambda: act(there))

    for load in loads:
        load.wait()
    weight[...] = volume[...] * jnp.exp(-LOG_STEP * exponent[...].astype(f32))
    y_layer[...] = weight[pl.ds(SPAN - 1, SPAN, stride=SPAN), :]
    last = one_hot(iota((8, LANES), 1) == LANES - 1)
    edge[...] = pick_t(last, weight[...])[0:1]

    @pl.when(is_root)
    def _():
        pl.semaphore_wait(barrier, DEV - 1)

    @pl.when(is_mid_root)
    def _():
        pl.semaphore_wait(barrier, DEV // 4 * 3 - 1)

    @pl.when(is_early_root)
    def _():
        pl.semaphore_wait(barrier, DEV // 2 - 1)

    @pl.when(not_(is_root | is_mid_root | is_early_root))
    def _():
        pl.semaphore_wait(barrier, len(HALO))

    halo_from = (
        weight.at[pl.ds(ROWS - SPAN, SPAN)], y_layer, weight.at[pl.ds(ROWS - 8, 8)],
        edge, edge, edge, edge,
    )
    halo_to = (
        lines_got.at[pl.ds(0, SPAN)], lines_got.at[pl.ds(SPAN, SPAN)],
        lines_got.at[pl.ds(2 * SPAN, 8)], *(z_got.at[n] for n in range(4)),
    )
    halos = []
    for n, step in enumerate(HALO):
        copy = pltpu.make_async_remote_copy(
            src_ref=halo_from[n], dst_ref=halo_to[n],
            send_sem=halo_send.at[n], recv_sem=halo_recv.at[n],
            device_id=ahead(*step), device_id_type=LOGICAL,
        )
        copy.start()
        halos.append(copy)

    @pl.when(is_early_root)
    def _():
        visit((0, 1), lambda there: signal(early_sem, there))

    @pl.when(is_mid_root)
    def _():
        visit((0, 1, 2), lambda there: signal(mid_sem, there), FIRST)

    @pl.when(is_root)
    def _():
        visit((0, 1, 3, 2), lambda there: signal(go_sem, there), FIRST)

    owner_dev = owner[...] // ROWS
    slots = (owner[...] - owner_dev * ROWS).astype(f32)
    same = owner_dev == iota((DEV, ROWS), 0)
    before = one_hot(iota((ROWS, ROWS), 0) < iota((ROWS, ROWS), 1))
    rank = dot_n(one_hot(same), before)
    ranked = [one_hot(same & (rank == value)) for value in (0.0, 1.0)]
    order = jnp.concatenate(ranked, axis=0)

    def put(part, rows):
        packed[2 * part] = rows[:DEV]
        packed[2 * part + 1] = rows[DEV:]

    own = weight[...].reshape(SPAN, SPAN, LANES)
    put(0, pick(order, weight[...]))

    def send(first, count):
        def act(there):
            pltpu.make_async_remote_copy(
                src_ref=packed.at[pl.ds(first, count), pl.ds(there, 1), :],
                dst_ref=got.at[pl.ds(first, count), pl.ds(my_dev, 1), :],
                send_sem=send_sem, recv_sem=recv_sem,
                device_id=there, device_id_type=LOGICAL,
            ).start()

        return act

    @pl.when(is_early & not_(is_early_root))
    def _():
        pl.semaphore_wait(early_sem, 1)

    @pl.when(is_mid & not_(is_mid_root))
    def _():
        pl.semaphore_wait(mid_sem, 1)

    @pl.when(is_late & not_(is_root))
    def _():
        pl.semaphore_wait(go_sem, 1)

    visit((0, 1), send(0, 2))

    empty = jnp.zeros((1, SPAN, LANES), f32)
    behind_x = jnp.concatenate([empty, own[:-1]], axis=0)
    column = jnp.zeros((SPAN, 1, LANES), f32)
    behind_y = jnp.concatenate([column, own[:, :-1]], axis=1)
    behind_xy = jnp.concatenate([column, behind_x[:, :-1]], axis=1)
    from_row, line = iota((ROWS, LANES), 0), iota((ROWS, LANES), 1)
    in_x, in_y = line < SPAN, (line >= SPAN) & (line < 2 * SPAN)
    wanted = (
        jnp.where(in_x, line, -1),
        jnp.where(in_y, (line - SPAN) * SPAN, -1),
        jnp.where(
            in_x & (line < SPAN - 1),
            line + 1,
            jnp.where(
                in_y & (line < 2 * SPAN - 1),
                (line - SPAN + 1) * SPAN,
                jnp.where(line == 2 * SPAN + 7, 0, -1),
            ),
        ),
    )
    selects = []
    for n, inner in enumerate((behind_x, behind_y, behind_xy)):
        put(n + 1, pick(order, inner.reshape(ROWS, LANES)))
        selects.append(dot_n(order, one_hot(from_row == wanted[n])).astype(bf16))
    select = jnp.concatenate(selects, axis=0)

    for copy in halos:
        copy.wait()

    pad = jnp.zeros((LANES - 2 * SPAN - 8, LANES), f32)
    rim = pick(select, jnp.concatenate([lines_got[...], pad], axis=0))
    for n in range(6):
        packed[n + 2] += rim[n * DEV : (n + 1) * DEV]

    at = iota((1, ROWS), 1)
    first_x, first_y = at < SPAN, at % SPAN == 0
    z_own, z_x, z_y, z_xy = (z_got[n] for n in range(4))

    def turn(row, by):
        return pltpu.roll(row, by % ROWS, 1)

    z_rows = (
        z_own,
        jnp.where(first_x, turn(z_x, SPAN), turn(z_own, SPAN)),
        jnp.where(first_y, turn(z_y, 1 - SPAN), turn(z_own, 1)),
        jnp.where(
            first_x,
            jnp.where(first_y, turn(z_xy, 1), turn(z_x, SPAN + 1)),
            jnp.where(first_y, turn(z_y, 1), turn(z_own, SPAN + 1)),
        ),
        slots,
    )
    table = jnp.zeros((8, ROWS), f32)
    for n, row in enumerate(z_rows):
        table = jnp.where(iota((8, ROWS), 0) == n, row, table)
    blank = jnp.zeros((LANES - 16, ROWS), f32)
    none = jnp.zeros((8, ROWS), f32)
    packed[8] = pick_t(ranked[0], jnp.concatenate([table, none, blank], axis=0)) + pick_t(
        ranked[1], jnp.concatenate([none, table, blank], axis=0)
    )

    keep = pltpu.make_async_copy(
        packed.at[:, pl.ds(my_dev, 1), :], got.at[:, pl.ds(my_dev, 1), :], own_sem
    )
    keep.start()
    visit((0, 1), send(2, PARTS - 2))

    @pl.when(is_early)
    def _():
        pl.semaphore_wait(mid_sem, 1)

    visit((2,), send(0, PARTS))

    @pl.when(not_(is_late))
    def _():
        pl.semaphore_wait(go_sem, 1)

    visit((3,), send(0, PARTS))
    keep.wait()
    all_others = pl.ds(0, DEV - 1)
    pltpu.make_async_remote_copy(
        src_ref=packed.at[:, all_others], dst_ref=got.at[:, all_others],
        send_sem=send_sem, recv_sem=recv_sem, device_id=my_dev, device_id_type=LOGICAL,
    ).wait()


def assemble(got, stencil_hbm, lumped_hbm, stencil, lumped, out_sems, lump_sem):
    rows = ROWS // CHUNKS
    extra = got[8]
    tails = [extra, pltpu.roll(extra, LANES - 8, 1)]
    slot = jnp.concatenate(
        [
            dot_t(one_hot(iota((8, LANES), 1) == 4), tail.astype(bf16))[0:1]
            for tail in tails
        ],
        axis=1,
    )
    five = [(got[2 * n], got[2 * n + 1]) for n in range(4)] + [tails]
    five = [jnp.concatenate(pieces(jnp.concatenate(two, axis=0)), axis=1) for two in five]
    lane = iota((rows, LANES), 1)
    copies = []
    for chunk in range(CHUNKS):
        here = pl.ds(chunk * rows, rows)
        mine = iota((rows, ROWS), 0) + chunk * rows
        place = one_hot(slot == mine.astype(f32), 0.015625)
        both = [dot_n(place, two) for two in five]
        placed = [pair[:, :LANES] + pair[:, LANES:] for pair in both]
        now, tail = placed[:4], placed[4]
        behind = [
            jnp.where(lane == 0, tail[:, n : n + 1], pltpu.roll(line, 1, 1))
            for n, line in enumerate(now)
        ]
        total = sum(now) + sum(behind)
        lumped[here, :] = 1.0 / (27.0 * total)

        def spread(current, back):
            return (back, 2.0 * (current + back), current)

        def plane(four):
            along = zip(spread(four[0], four[1]), spread(four[2], four[3]))
            return [value for current, back in along for value in spread(current, back)]

        for n, (current, back) in enumerate(zip(plane(now), plane(behind))):
            for k, value in enumerate(spread(current, back)):
                stencil[3 * n + k, here, :] = value
        copy = pltpu.make_async_copy(
            stencil.at[:, here], stencil_hbm.at[:, here], out_sems.at[chunk]
        )
        copy.start()
        copies.append(copy)
    copy = pltpu.make_async_copy(lumped, lumped_hbm, lump_sem)
    copy.start()
    copies.append(copy)
    for copy in copies:
        copy.wait()


def in_hbm(x):
    return pltpu.with_memory_space_constraint(x, pltpu.HBM)


def shards(cell_volume, exponent, owner_row):
    vmem = pl.BlockSpec(memory_space=pltpu.VMEM)
    hbm = pl.BlockSpec(memory_space=pltpu.HBM)
    dma, regular = pltpu.SemaphoreType.DMA, pltpu.SemaphoreType.REGULAR
    got = pl.pallas_call(
        exchange,
        name="exchange",
        out_shape=pltpu.VMEM((PARTS, DEV, LANES), f32),
        in_specs=[hbm] * 3,
        out_specs=vmem,
        scratch_shapes=[
            pltpu.VMEM((ROWS, LANES), f32),
            pltpu.VMEM((ROWS, LANES), i32),
            pltpu.VMEM((1, ROWS), i32),
            pltpu.VMEM((ROWS, LANES), f32),
            pltpu.VMEM((SPAN, LANES), f32),
            pltpu.VMEM((1, ROWS), f32),
            pltpu.VMEM((2 * SPAN + 8, LANES), f32),
            pltpu.VMEM((4, 1, ROWS), f32),
            pltpu.VMEM((PARTS, DEV, LANES), f32),
            dma((3,)), dma((7,)), dma((7,)), dma, dma, dma, regular, regular, regular,
        ],
        compiler_params=pltpu.CompilerParams(
            has_side_effects=True, collective_id=1, vmem_limit_bytes=16 << 20
        ),
    )(
        in_hbm(cell_volume.reshape(ROWS, LANES)),
        in_hbm(exponent.reshape(ROWS, LANES)),
        in_hbm(owner_row.reshape(1, ROWS)),
    )
    return pl.pallas_call(
        assemble,
        name="assemble",
        out_shape=(
            jax.ShapeDtypeStruct((27, ROWS, LANES), f32),
            jax.ShapeDtypeStruct((ROWS, LANES), f32),
        ),
        in_specs=[vmem],
        out_specs=(hbm, hbm),
        scratch_shapes=[
            pltpu.VMEM((27, ROWS, LANES), f32),
            pltpu.VMEM((ROWS, LANES), f32),
            dma((CHUNKS,)), dma,
        ],
        compiler_params=pltpu.CompilerParams(vmem_limit_bytes=16 << 20),
    )(got)


def solution(mesh):
    return jax.shard_map(
        shards,
        mesh=mesh,
        in_specs=(P(*AXES), P(*AXES), P(AXES)),
        out_specs=(P(None, AXES, None), P(AXES, None)),
        check_vma=False,
    )
```

time: 27.2 us -> 24.3 us (0.89); the launches traced: 26.7 us -> 24.2 us
  Pallas kernels: 26 us -> 23.5 us
    pallas_call x1, Pallas kernels: 23 us -> 21 us  [shards(): pl.pallas_call(exchange, name='exchange', out_shape=pltpu.VMEM((PARTS, DE...]
    pallas_call x1, Pallas kernels: 3.04 us -> 2.54 us  [shards(): pl.pallas_call(assemble, name='assemble', out_shape=(jax.ShapeDtypeStruct...]
where the time goes in v3:
time: 24.3 us; the launch traced here: 24.2 us
  Pallas kernels  23.5 us (97%)
  between operations  0.64 us (3%)
    pallas_call x1, Pallas kernels, shards(): pl.pallas_call(exchange, name='exchange', out_shape=pltpu.VMEM((PARTS, DE...  21 us
    pallas_call x1, Pallas kernels, shards(): pl.pallas_call(assemble, name='assemble', out_shape=(jax.ShapeDtypeStruct...  2.54 us

profile of v3, /device:TPU:1, one launch (start us, length us, event | category | flops | bytes accessed | tf_op | source)
XLA Modules:
  0.0 24.2 jit_solution(12146589668014198953)
XLA Ops:
  0.6 21.0 %exchange.1.got = f32[9,128,128]{2,1,0:T(8,128)S(1)} custom-call(f32[256,128]{1,0:T(8,128)} %bitcast.3, s32[256,128]{1,0:T(8,128)} %bitcast.4, s32[1,256]{1,0:T(1,128)} %bitcast.5), custom_call_target="tpu_custom_call" | custom-call | tf_op jit(solution)/shard_map/exchange/pallas_call | solution.py:372
  21.6 2.5 %assemble.1 = (f32[27,256,128]{2,1,0:T(8,128)}, f32[256,128]{1,0:T(8,128)}) custom-call(f32[9,128,128]{2,1,0:T(8,128)S(1)} %exchange.1.got), custom_call_target="tpu_custom_call" | custom-call | tf_op jit(solution)/shard_map/assemble/pallas_call | solution.py:398

commit v4 on v3

--- a/solution.py
+++ b/solution.py
@@ -20,6 +20,7 @@
 ROWS = SPAN * SPAN
 LANES = 128
 PARTS = 9
+STRIDE = 13
 CHUNKS = 4
 HALO = ((1, 0, 0), (0, 1, 0), (1, 1, 0), (0, 0, 1), (1, 0, 1), (0, 1, 1), (1, 1, 1))
 
@@ -104,32 +105,39 @@
     for source in sources:
         signal(barrier, source)
 
-    def plane(number):
-        z_hi, z_lo = number // 2, number % 2
+    def members(planes, side=None):
+        z_hi, z_lo = planes[0] // 2, planes[0] % 2
         core, y = lax.rem(me[0], 2), lax.rem(me[1], HALF)
-        base_x = [(z_lo * 2 + lax.rem(core + k, 2)) * (NY * NZ) for k in range(2)]
-        base_y = [(z_hi * HALF + lax.rem(y + k, HALF)) * NZ for k in range(HALF)]
+        if len(planes) == 2:
+            base_x = [lax.rem(me[0] + k, NX) * (NY * NZ) for k in range(NX)]
+            at_home = me[1] // HALF == z_hi
+        else:
+            base_x = [(z_lo * 2 + lax.rem(core + k, 2)) * (NY * NZ) for k in range(2)]
+            at_home = my_plane == planes[0]
+        if side is None:
+            base_y = [(z_hi * HALF + lax.rem(y + k, HALF)) * NZ for k in range(HALF)]
+        else:
+            base_y = [(z_hi * HALF + side * 2 + lax.rem(y + k, 2)) * NZ for k in range(2)]
+            at_home = at_home & (y // 2 == side)
         base_z = [lax.rem(me[2] + k, NZ) for k in range(NZ)]
-        members = 2 * HALF * NZ
-        here = my_plane == number
-        for n in range(members):
-            step = n * 13 % members
-            there = base_x[step % 2] + base_y[step // 2 % HALF] + base_z[step // (2 * HALF)]
-            yield (here if step == 0 else None), there
-
-    def visit(planes, act, first=()):
+        bases = [(x, y) for y in base_y for x in base_x]
+        count = len(bases) * NZ
+        for n in range(count):
+            step = n * STRIDE % count
+            x, y = bases[step % len(bases)]
+            yield (at_home if step == 0 else None), x + y + base_z[step // len(bases)]
+
+    def visit(planes, act, first=(), side=None):
         for there in first:
             pl.when(my_dev != there)(lambda: act(jnp.int32(there)))
-        for number in planes:
-            for self_at, there in plane(number):
-                go = None if self_at is None else not_(self_at)
-                if number == 0:
-                    for known in first:
-                        go = there != known if go is None else go & (there != known)
-                if go is None:
-                    act(there)
-                else:
-                    pl.when(go)(lambda: act(there))
+        for self_at, there in members(planes, side):
+            go = None if self_at is None else not_(self_at)
+            for known in first:
+                go = there != known if go is None else go & (there != known)
+            if go is None:
+                act(there)
+            else:
+                pl.when(go)(lambda: act(there))
 
     for load in loads:
         load.wait()
@@ -178,11 +186,14 @@
 
     @pl.when(is_mid_root)
     def _():
-        visit((0, 1, 2), lambda there: signal(mid_sem, there), FIRST)
+        visit((0, 1), lambda there: signal(mid_sem, there), FIRST)
+        visit((2,), lambda there: signal(mid_sem, there))
 
     @pl.when(is_root)
     def _():
-        visit((0, 1, 3, 2), lambda there: signal(go_sem, there), FIRST)
+        visit((3,), lambda there: signal(go_sem, there))
+        visit((0, 1), lambda there: signal(go_sem, there), FIRST)
+        visit((2,), lambda there: signal(go_sem, there))
 
     owner_dev = owner[...] // ROWS
     slots = (owner[...] - owner_dev * ROWS).astype(f32)
@@ -223,6 +234,19 @@
         pl.semaphore_wait(go_sem, 1)
 
     visit((0, 1), send(0, 2))
+
+    @pl.when(is_early)
+    def _():
+        pl.semaphore_wait(mid_sem, 1)
+
+    visit((2,), send(0, 2))
+
+    @pl.when(not_(is_late))
+    def _():
+        pl.semaphore_wait(go_sem, 1)
+
+    visit((3,), send(0, 2))
+
 
     empty = jnp.zeros((1, SPAN, LANES), f32)
     behind_x = jnp.concatenate([empty, own[:-1]], axis=0)
@@ -291,17 +315,9 @@
     keep.start()
     visit((0, 1), send(2, PARTS - 2))
 
-    @pl.when(is_early)
-    def _():
-        pl.semaphore_wait(mid_sem, 1)
-
-    visit((2,), send(0, PARTS))
-
-    @pl.when(not_(is_late))
-    def _():
-        pl.semaphore_wait(go_sem, 1)
-
-    visit((3,), send(0, PARTS))
+    visit((2,), send(2, PARTS - 2))
+
+    visit((3,), send(2, PARTS - 2))
     keep.wait()
     all_others = pl.ds(0, DEV - 1)
     pltpu.make_async_remote_copy(

time: 24.3 us -> 23.6 us (0.971)
  Pallas kernels: 23.5 us -> 22.8 us
    pallas_call x1, Pallas kernels: 21 us -> 20.3 us  [shards(): pl.pallas_call(exchange, name='exchange', out_shape=pltpu.VMEM((PARTS, DE...]
where the time goes in v4:
time: 23.6 us; the launch traced here: 23.5 us
  Pallas kernels  22.8 us (97%)
  between operations  0.64 us (3%)
    pallas_call x1, Pallas kernels, shards(): pl.pallas_call(exchange, name='exchange', out_shape=pltpu.VMEM((PARTS, DE...  20.3 us
    pallas_call x1, Pallas kernels, shards(): pl.pallas_call(assemble, name='assemble', out_shape=(jax.ShapeDtypeStruct...  2.54 us

profile of v4, /device:TPU:1, one launch (start us, length us, event | category | flops | bytes accessed | tf_op | source)
XLA Modules:
  0.0 23.5 jit_solution(740082827297496689)
XLA Ops:
  0.6 20.3 %exchange.1.got = f32[9,128,128]{2,1,0:T(8,128)S(1)} custom-call(f32[256,128]{1,0:T(8,128)} %bitcast.3, s32[256,128]{1,0:T(8,128)} %bitcast.4, s32[1,256]{1,0:T(1,128)} %bitcast.5), custom_call_target="tpu_custom_call" | custom-call | tf_op jit(solution)/shard_map/exchange/pallas_call | solution.py:388
  20.9 2.5 %assemble.1 = (f32[27,256,128]{2,1,0:T(8,128)}, f32[256,128]{1,0:T(8,128)}) custom-call(f32[9,128,128]{2,1,0:T(8,128)S(1)} %exchange.1.got), custom_call_target="tpu_custom_call" | custom-call | tf_op jit(solution)/shard_map/assemble/pallas_call | solution.py:414

commit v5 on v4

--- a/solution.py
+++ b/solution.py
@@ -221,33 +221,6 @@
 
         return act
 
-    @pl.when(is_early & not_(is_early_root))
-    def _():
-        pl.semaphore_wait(early_sem, 1)
-
-    @pl.when(is_mid & not_(is_mid_root))
-    def _():
-        pl.semaphore_wait(mid_sem, 1)
-
-    @pl.when(is_late & not_(is_root))
-    def _():
-        pl.semaphore_wait(go_sem, 1)
-
-    visit((0, 1), send(0, 2))
-
-    @pl.when(is_early)
-    def _():
-        pl.semaphore_wait(mid_sem, 1)
-
-    visit((2,), send(0, 2))
-
-    @pl.when(not_(is_late))
-    def _():
-        pl.semaphore_wait(go_sem, 1)
-
-    visit((3,), send(0, 2))
-
-
     empty = jnp.zeros((1, SPAN, LANES), f32)
     behind_x = jnp.concatenate([empty, own[:-1]], axis=0)
     column = jnp.zeros((SPAN, 1, LANES), f32)
@@ -273,14 +246,50 @@
         put(n + 1, pick(order, inner.reshape(ROWS, LANES)))
         selects.append(dot_n(order, one_hot(from_row == wanted[n])).astype(bf16))
     select = jnp.concatenate(selects, axis=0)
-
-    for copy in halos:
+    select = jnp.concatenate([select, select], axis=1)
+
+    halos[0].wait()
+    pad = jnp.zeros((LANES - SPAN, LANES), f32)
+    x_lines = jnp.concatenate([lines_got[0:SPAN], pad], axis=0)
+    rim = dot_n(select[:ROWS], jnp.concatenate(pieces(x_lines), axis=0))
+    for n in range(2):
+        packed[n + 2] += rim[n * DEV : (n + 1) * DEV]
+
+    @pl.when(is_early & not_(is_early_root))
+    def _():
+        pl.semaphore_wait(early_sem, 1)
+
+    @pl.when(is_mid & not_(is_mid_root))
+    def _():
+        pl.semaphore_wait(mid_sem, 1)
+
+    @pl.when(is_late & not_(is_root))
+    def _():
+        pl.semaphore_wait(go_sem, 1)
+
+    visit((0, 1), send(0, 4))
+
+    @pl.when(is_early & not_(is_mid_root))
+    def _():
+        pl.semaphore_wait(mid_sem, 1)
+
+    visit((2,), send(0, 4))
+
+    @pl.when(not_(is_late))
+    def _():
+        pl.semaphore_wait(go_sem, 1)
+
+    visit((3,), send(0, 4))
+
+
+    for copy in halos[1:]:
         copy.wait()
 
     pad = jnp.zeros((LANES - 2 * SPAN - 8, LANES), f32)
-    rim = pick(select, jnp.concatenate([lines_got[...], pad], axis=0))
-    for n in range(6):
-        packed[n + 2] += rim[n * DEV : (n + 1) * DEV]
+    rim_lines = jnp.concatenate([lines_got[...], pad], axis=0)
+    rim = dot_n(select[ROWS:], jnp.concatenate(pieces(rim_lines), axis=0))
+    for n in range(4):
+        packed[n + 4] += rim[n * DEV : (n + 1) * DEV]
 
     at = iota((1, ROWS), 1)
     first_x, first_y = at < SPAN, at % SPAN == 0
@@ -303,21 +312,23 @@
     table = jnp.zeros((8, ROWS), f32)
     for n, row in enumerate(z_rows):
         table = jnp.where(iota((8, ROWS), 0) == n, row, table)
-    blank = jnp.zeros((LANES - 16, ROWS), f32)
-    none = jnp.zeros((8, ROWS), f32)
-    packed[8] = pick_t(ranked[0], jnp.concatenate([table, none, blank], axis=0)) + pick_t(
-        ranked[1], jnp.concatenate([none, table, blank], axis=0)
+    high, low = pieces(table)
+    none = jnp.zeros((16, ROWS), bf16)
+    blank = jnp.zeros((LANES - 32, ROWS), bf16)
+    both = jnp.concatenate([high, low], axis=0)
+    packed[8] = dot_t(ranked[0], jnp.concatenate([both, none, blank], axis=0)) + dot_t(
+        ranked[1], jnp.concatenate([none, both, blank], axis=0)
     )
 
     keep = pltpu.make_async_copy(
         packed.at[:, pl.ds(my_dev, 1), :], got.at[:, pl.ds(my_dev, 1), :], own_sem
     )
     keep.start()
-    visit((0, 1), send(2, PARTS - 2))
-
-    visit((2,), send(2, PARTS - 2))
-
-    visit((3,), send(2, PARTS - 2))
+    visit((0, 1), send(4, PARTS - 4), FIRST)
+
+    visit((2,), send(4, PARTS - 4))
+
+    visit((3,), send(4, PARTS - 4))
     keep.wait()
     all_others = pl.ds(0, DEV - 1)
     pltpu.make_async_remote_copy(
@@ -329,7 +340,8 @@
 def assemble(got, stencil_hbm, lumped_hbm, stencil, lumped, out_sems, lump_sem):
     rows = ROWS // CHUNKS
     extra = got[8]
-    tails = [extra, pltpu.roll(extra, LANES - 8, 1)]
+    extra += pltpu.roll(extra, LANES - 8, 1)
+    tails = [extra, pltpu.roll(extra, LANES - 16, 1)]
     slot = jnp.concatenate(
         [
             dot_t(one_hot(iota((8, LANES), 1) == 4), tail.astype(bf16))[0:1]

time: 23.6 us -> 23.1 us (0.979)
  Pallas kernels: 22.8 us -> 22.4 us
    pallas_call x1, Pallas kernels: 20.3 us -> 19.8 us  [shards(): pl.pallas_call(exchange, name='exchange', out_shape=pltpu.VMEM((PARTS, DE...]
where the time goes in v5:
time: 23.1 us; the launch traced here: 23 us
  Pallas kernels  22.4 us (97%)
  between operations  0.64 us (3%)
    pallas_call x1, Pallas kernels, shards(): pl.pallas_call(exchange, name='exchange', out_shape=pltpu.VMEM((PARTS, DE...  19.8 us
    pallas_call x1, Pallas kernels, shards(): pl.pallas_call(assemble, name='assemble', out_shape=(jax.ShapeDtypeStruct...  2.6 us

profile of v5, /device:TPU:1, one launch (start us, length us, event | category | flops | bytes accessed | tf_op | source)
XLA Modules:
  0.0 23.0 jit_solution(2251921706538707772)
XLA Ops:
  0.6 19.8 %exchange.1.got = f32[9,128,128]{2,1,0:T(8,128)S(1)} custom-call(f32[256,128]{1,0:T(8,128)} %bitcast.3, s32[256,128]{1,0:T(8,128)} %bitcast.4, s32[1,256]{1,0:T(1,128)} %bitcast.5), custom_call_target="tpu_custom_call" | custom-call | tf_op jit(solution)/shard_map/exchange/pallas_call | solution.py:400
  20.4 2.6 %assemble.1 = (f32[27,256,128]{2,1,0:T(8,128)}, f32[256,128]{1,0:T(8,128)}) custom-call(f32[9,128,128]{2,1,0:T(8,128)S(1)} %exchange.1.got), custom_call_target="tpu_custom_call" | custom-call | tf_op jit(solution)/shard_map/assemble/pallas_call | solution.py:426

commit v6 on v5

--- a/solution.py
+++ b/solution.py
@@ -267,7 +267,7 @@
     def _():
         pl.semaphore_wait(go_sem, 1)
 
-    visit((0, 1), send(0, 4))
+    visit((0, 1), send(0, 4), FIRST)
 
     @pl.when(is_early & not_(is_mid_root))
     def _():

time: 23.1 us -> 23 us (level)
  no operation moved by 1% of the time
where the time goes in v6:
time: 23 us; the launch traced here: 22.9 us
  Pallas kernels  22.3 us (97%)
  between operations  0.64 us (3%)
    pallas_call x1, Pallas kernels, shards(): pl.pallas_call(exchange, name='exchange', out_shape=pltpu.VMEM((PARTS, DE...  19.7 us
    pallas_call x1, Pallas kernels, shards(): pl.pallas_call(assemble, name='assemble', out_shape=(jax.ShapeDtypeStruct...  2.6 us

profile of v6, /device:TPU:1, one launch (start us, length us, event | category | flops | bytes accessed | tf_op | source)
XLA Modules:
  0.0 22.9 jit_solution(17506909498090828916)
XLA Ops:
  0.6 19.7 %exchange.1.got = f32[9,128,128]{2,1,0:T(8,128)S(1)} custom-call(f32[256,128]{1,0:T(8,128)} %bitcast.3, s32[256,128]{1,0:T(8,128)} %bitcast.4, s32[1,256]{1,0:T(1,128)} %bitcast.5), custom_call_target="tpu_custom_call" | custom-call | tf_op jit(solution)/shard_map/exchange/pallas_call | solution.py:400
  20.3 2.6 %assemble.1 = (f32[27,256,128]{2,1,0:T(8,128)}, f32[256,128]{1,0:T(8,128)}) custom-call(f32[9,128,128]{2,1,0:T(8,128)S(1)} %exchange.1.got), custom_call_target="tpu_custom_call" | custom-call | tf_op jit(solution)/shard_map/assemble/pallas_call | solution.py:426

commit v7 on v6

--- a/solution.py
+++ b/solution.py
@@ -20,7 +20,7 @@
 ROWS = SPAN * SPAN
 LANES = 128
 PARTS = 9
-STRIDE = 13
+STRIDE = 19
 CHUNKS = 4
 HALO = ((1, 0, 0), (0, 1, 0), (1, 1, 0), (0, 0, 1), (1, 0, 1), (0, 1, 1), (1, 1, 1))
 

time: 23 us -> 23 us (level)
  no operation moved by 1% of the time
where the time goes in v7:
time: 23 us; the launch traced here: 22.9 us
  Pallas kernels  22.3 us (97%)
  between operations  0.64 us (3%)
    pallas_call x1, Pallas kernels, shards(): pl.pallas_call(exchange, name='exchange', out_shape=pltpu.VMEM((PARTS, DE...  19.7 us
    pallas_call x1, Pallas kernels, shards(): pl.pallas_call(assemble, name='assemble', out_shape=(jax.ShapeDtypeStruct...  2.6 us

profile of v7, /device:TPU:1, one launch (start us, length us, event | category | flops | bytes accessed | tf_op | source)
XLA Modules:
  0.0 22.9 jit_solution(7211271604758328170)
XLA Ops:
  0.6 19.7 %exchange.1.got = f32[9,128,128]{2,1,0:T(8,128)S(1)} custom-call(f32[256,128]{1,0:T(8,128)} %bitcast.3, s32[256,128]{1,0:T(8,128)} %bitcast.4, s32[1,256]{1,0:T(1,128)} %bitcast.5), custom_call_target="tpu_custom_call" | custom-call | tf_op jit(solution)/shard_map/exchange/pallas_call | solution.py:400
  20.3 2.6 %assemble.1 = (f32[27,256,128]{2,1,0:T(8,128)}, f32[256,128]{1,0:T(8,128)}) custom-call(f32[9,128,128]{2,1,0:T(8,128)S(1)} %exchange.1.got), custom_call_target="tpu_custom_call" | custom-call | tf_op jit(solution)/shard_map/assemble/pallas_call | solution.py:426
